TPU v7x, 32 devices: a whole 2x2x4 slice. The times are simulated.
32 devices in a mesh: mom: 4 (over y, core), tm: 4 (over z), pt: 2 (over x).
Axes of the slice: x: 2, y: 2, z: 4, core: 2. Of those that a mesh axis runs over, the one named last changes fastest.
Arguments:
- chi_time: bfloat16 [16, 8, 896, 896], P('tm', 'mom', 'pt'), may hold values from -4 to 4
- green: bfloat16 [8, 16, 896, 896], P('mom', 'tm', 'pt'), may hold values from -6 to 6
- band_coeffs: bfloat16 [896, 1024], replicated, may hold values from -1 to 1
Outputs:
- self_energy: float32 [8, 16, 1024], P('mom', 'tm', 'pt')
All inputs are finite; a program needn't handle non-finite values.
Results may differ from a plain program's by a relative error of at most 0.009.
Values may be sent and summed in bfloat16 or wider, within the bound.
A program may use at most 128 MiB of HBM per device.

v0:
```python
import math

import jax
import jax.numpy as jnp
from jax import lax
from jax.sharding import Mesh, PartitionSpec as P

COUPLING = 0.8
JOINT = True


def cosine_table(count):
    index = jnp.arange(count, dtype=jnp.float32) + 0.5
    angle = jnp.pi * index[:, None] * index[None, :] / count
    return (jnp.sqrt(jnp.float32(2.0 / count)) * jnp.cos(angle)).astype(jnp.bfloat16)


def hartley_table(count):
    index = jnp.arange(count, dtype=jnp.float32)
    angle = 2.0 * jnp.pi * index[:, None] * index[None, :] / count
    return (jnp.cos(angle) + jnp.sin(angle)) / jnp.sqrt(jnp.float32(count))


def product(left, right):
    return jnp.einsum("apq,aqs->aps", left, right, preferred_element_type=jnp.float32)


def series(tiles):
    square = product(tiles, tiles).astype(jnp.bfloat16)
    two = (tiles.astype(jnp.float32) + square.astype(jnp.float32)).astype(jnp.bfloat16)
    fourth = product(square, square).astype(jnp.bfloat16)
    four = (two.astype(jnp.float32) + product(two, square)).astype(jnp.bfloat16)
    return (four.astype(jnp.float32) + product(four, fourth)).astype(jnp.bfloat16)


def local(chi_time, green, band_coeffs):
    times_dev, moms_dev, rows_dev, points = chi_time.shape
    momenta, high, low = lax.axis_size("mom"), lax.axis_size("th"), lax.axis_size("tl")
    count_t = times_dev * high * low
    count_k = moms_dev * momenta
    part = rows_dev // low
    piece = part // momenta
    own_k = moms_dev // high
    cosine = cosine_table(count_t)
    hartley = hartley_table(count_k).astype(jnp.bfloat16)
    scale = COUPLING / math.sqrt(points)

    cells_dev = green.shape[0]
    spread = green.reshape(cells_dev, times_dev, low, momenta, piece, points)
    spread = spread.transpose(3, 0, 1, 2, 4, 5)
    spread = lax.all_to_all(spread, "mom", split_axis=0, concat_axis=0, tiled=True)
    spread = spread.reshape(count_k, times_dev, low, piece, points)

    blocks = chi_time.reshape(times_dev, high, own_k, low, part, points)
    blocks = blocks.transpose(1, 3, 0, 2, 4, 5).reshape(high * low, times_dev * own_k, part, points)
    blocks = lax.all_to_all(blocks, ("th", "tl"), split_axis=0, concat_axis=0, tiled=True)
    blocks = blocks.reshape(count_t, own_k, part, points)
    mixed = jnp.einsum("wt,tkpq->wkpq", cosine, blocks, preferred_element_type=jnp.float32)
    mixed = (scale * mixed).astype(jnp.bfloat16).reshape(count_t * own_k, part, points)
    tiles = lax.all_to_all(mixed, ("pt", "tl"), split_axis=0, concat_axis=1, tiled=True)
    screened = series(tiles)
    back = lax.all_to_all(screened, ("pt", "tl"), split_axis=1, concat_axis=0, tiled=True)
    back = back.reshape(count_t, own_k, part, points)
    timed = jnp.einsum("tw,wkpq->tkpq", cosine, back, preferred_element_type=jnp.float32)
    timed = timed.astype(jnp.bfloat16)

    if JOINT:
        timed = timed.reshape(high * low, times_dev, own_k, momenta, piece, points)
        timed = timed.transpose(3, 0, 1, 2, 4, 5)
        timed = timed.reshape(momenta * high * low, times_dev, own_k, piece, points)
        timed = lax.all_to_all(timed, ("mom", "th", "tl"), split_axis=0, concat_axis=0, tiled=True)
    else:
        timed = timed.reshape(high * low, times_dev, own_k, part, points)
        timed = lax.all_to_all(timed, ("th", "tl"), split_axis=0, concat_axis=0, tiled=True)
        timed = timed.reshape(high * low, times_dev, own_k, momenta, piece, points)
        timed = timed.transpose(3, 0, 1, 2, 4, 5)
        timed = lax.all_to_all(timed, "mom", split_axis=0, concat_axis=0, tiled=True)
    timed = timed.reshape(momenta, high, low, times_dev, own_k, piece, points)
    timed = timed.transpose(0, 1, 4, 3, 2, 5, 6).reshape(count_k, times_dev, low, piece, points)
    lattice = jnp.einsum("rk,ktlpq->rtlpq", hartley, timed, preferred_element_type=jnp.float32)
    sigma = (spread.astype(jnp.float32) * lattice).astype(jnp.bfloat16)

    own = lax.dynamic_slice_in_dim(band_coeffs, lax.axis_index("pt") * rows_dev, rows_dev, 0)
    own = own.reshape(low, momenta, piece, -1)
    own = lax.dynamic_index_in_dim(own, lax.axis_index("mom"), 1, keepdims=False)
    applied = jnp.einsum("rtlpq,qn->rtlpn", sigma, band_coeffs, preferred_element_type=jnp.float32)
    partial_sums = jnp.sum(applied * own.astype(jnp.float32)[None, None], axis=(2, 3))
    partial_sums = lax.psum_scatter(partial_sums, "mom", scatter_dimension=0, tiled=True)
    return lax.psum_scatter(partial_sums, "pt", scatter_dimension=2, tiled=True)


def solution(mesh):
    sizes = dict(mesh.shape)
    names, extents = [], []
    for name in mesh.axis_names:
        if name == "tm":
            names += ["th", "tl"]
            extents += [2, sizes[name] // 2]
        else:
            names.append(name)
            extents.append(sizes[name])
    fine = Mesh(mesh.devices.reshape(extents), tuple(names))
    tm = ("th", "tl")
    placed = (P(tm, "mom", "pt", None), P("mom", tm, "pt", None), P())
    return jax.shard_map(
        local, mesh=fine, in_specs=placed, out_specs=P("mom", tm, "pt"), check_vma=False
    )
```

profile of v0, /device:TPU:0, one launch (start us, length us, event | category | flops | bytes accessed | tf_op | source)
XLA Modules:
  0.0 738.9 jit_solution(15087316992124508674)
XLA Ops:
  6.5 0.0 copy-start
  6.5 10.6 %copy.26 = bf16[4,2,1,2,224,896]{5,0,4,3,1,2:T(4,128)(2,1)} copy(bf16[4,2,1,2,224,896]{5,4,3,1,0,2:T(8,128)(2,1)} %bitcast.70) | data formatting | bytes 12845056 | tf_op jit(solution)/shard_map/reshape | solution.py:54
  17.1 6.3 all-to-all-start.1
  23.5 141.6 %all-to-all-done.1 = bf16[4,4,224,896]{3,1,2,0:T(4,128)(2,1)} async-done(((bf16[4,4,224,896]{3,1,2,0:T(4,128)(2,1)}), bf16[4,4,224,896]{3,1,2,0:T(4,128)(2,1)}, u32[]{:S(2)}, u32[]{:S(2)}) %all-to-all-start.1) | async-done | bytes 6422560 | tf_op jit(solution)/shard_map/all_to_all | solution.py:56
  165.0 7.7 %copy.27 = bf16[4,4,224,896]{3,1,0,2:T(4,128)(2,1)} copy(bf16[4,4,224,896]{3,1,2,0:T(4,128)(2,1)} %all-to-all-done.1) | data formatting | bytes 12845056 | tf_op jit(solution)/shard_map/all_to_all | solution.py:56
  172.7 11.0 %reshape.71 = bf16[16,224,896]{2,0,1:T(8,128)(2,1)} reshape(bf16[4,4,224,896]{3,1,0,2:T(4,128)(2,1)} %copy.27) | data formatting | bytes 12845056 | tf_op jit(solution)/shard_map/reshape
  183.7 4.7 multiply_convert_fusion
  188.4 1.3 copy.28
  189.8 74.2 %all_to_all.48 = bf16[16,224,896]{2,1,0:T(8,128)(2,1)S(1)} all-to-all(bf16[16,224,896]{2,1,0:T(8,128)(2,1)S(1)} %copy.28), channel_id=1, replica_groups=mesh['mom'=4,'th'=2,'tl'=2,'pt'=2] {'pt','tl'}, dimensions={0} | all-to-all | bytes 12845056 | tf_op jit(solution)/shard_map/all_to_all | solution.py:60
  264.0 0.7 copy.29
  264.7 0.0 copy-start.1
  264.7 2.6 copy-done.1
  267.3 9.6 %convolution_convert_fusion.1 = bf16[4,896,896]{2,1,0:T(8,128)(2,1)} fusion(bf16[4,896,896]{2,1,0:T(8,128)(2,1)S(1)} %bitcast.72), kind=kOutput, calls=%fused_computation.13 | convolution fusion | flops 5757796352 | bytes 12845056 | tf_op jit(solution)/shard_map/apq,aqs->aps/dot_general | solution.py:25
  277.0 16.0 %add_convert_fusion.1 = bf16[4,896,896]{2,1,0:T(8,128)(2,1)} fusion(bf16[4,896,896]{2,1,0:T(8,128)(2,1)} %convolution_convert_fusion.1, bf16[4,896,896]{2,1,0:T(8,128)(2,1)} %bitcast.73), kind=kOutput, calls=%fused_computation.4 | convolution fusion | flops 5789908992 | bytes 19267584 | tf_op jit(solution)/shard_map/apq,aqs->aps/dot_general | solution.py:25
  293.0 25.1 %add_convert_fusion = bf16[4,896,896]{2,1,0:T(8,128)(2,1)} fusion(bf16[4,896,896]{2,1,0:T(8,128)(2,1)} %add_convert_fusion.1, bf16[4,896,896]{2,1,0:T(8,128)(2,1)} %convolution_convert_fusion.1), kind=kOutput, calls=%fused_computation.3 | convolution fusion | flops 11522015232 | bytes 19267584 | tf_op jit(solution)/shard_map/apq,aqs->aps/dot_general | solution.py:25
  318.1 10.5 %copy.30 = bf16[4,896,896]{2,0,1:T(4,128)(2,1)} copy(bf16[4,896,896]{2,1,0:T(8,128)(2,1)} %add_convert_fusion) | data formatting | bytes 12845056 | tf_op jit(solution)/shard_map/convert_element_type | solution.py:33
  328.6 5.3 all-to-all-start.3
  333.9 6.2 copy.24
  340.1 63.6 %all-to-all-done.3 = bf16[4,896,896]{2,0,1:T(4,128)(2,1)} async-done(((bf16[4,896,896]{2,0,1:T(4,128)(2,1)}), bf16[4,896,896]{2,0,1:T(4,128)(2,1)}, u32[]{:S(2)}, u32[]{:S(2)}) %all-to-all-start.3) | async-done | bytes 6422560 | tf_op jit(solution)/shard_map/all_to_all | solution.py:62
  403.6 5.5 all-to-all-start
  409.2 7.7 %copy.49 = bf16[4,4,224,896]{3,0,1,2:T(4,128)(2,1)} copy(bf16[4,4,224,896]{3,0,2,1:T(4,128)(2,1)} %bitcast.13) | data formatting | bytes 12845056 | tf_op jit(solution)/shard_map/all_to_all | solution.py:62
  416.9 11.0 %reshape.72 = bf16[16,224,896]{2,0,1:T(8,128)(2,1)} reshape(bf16[4,4,224,896]{3,1,0,2:T(4,128)(2,1)} %bitcast.68) | data formatting | bytes 12845056 | tf_op jit(solution)/shard_map/reshape.3
  427.9 7.4 %convolution_convert_fusion = bf16[16,224,896]{2,0,1:T(8,128)(2,1)} fusion(bf16[16,224,896]{2,0,1:T(8,128)(2,1)} %reshape.72, f32[16]{0:T(128)S(1)} %get-tuple-element.5, f32[16]{0:T(128)S(1)} %get-tuple-element.6), kind=kOutput, calls=%fused_computation.7 | convolution fusion | flops 105972736 | bytes 12845184 | tf_op jit(solution)/shard_map/tw,wkpq->tkpq/dot_general | solution.py:64
  435.3 11.5 %reshape.73 = bf16[4,4,1,4,56,896]{5,1,0,4,3,2:T(4,128)(2,1)} reshape(bf16[16,224,896]{2,0,1:T(8,128)(2,1)} %convolution_convert_fusion) | data formatting | bytes 12845056 | tf_op jit(solution)/shard_map/reshape | solution.py:68
  446.8 6.9 copy.32
  453.7 27.5 %all-to-all-done = bf16[4,2,4,2,56,896]{5,4,3,2,1,0:T(8,128)(2,1)} async-done(((bf16[4,2,4,2,56,896]{5,4,3,2,1,0:T(8,128)(2,1)}), bf16[4,2,4,2,56,896]{5,4,3,2,1,0:T(8,128)(2,1)}, u32[]{:S(2)}, u32[]{:S(2)}) %all-to-all-start) | async-done | bytes 6422560 | tf_op jit(solution)/shard_map/all_to_all | solution.py:51
  481.2 4.7 all-to-all-start.4
  485.9 0.0 all-reduce.3.cloned.1.call-start
  486.0 0.0 copy-done
  486.0 0.1 constant_dynamic-slice_fusion.1
  486.1 8.6 %bitcast_convert_fusion = f32[8,4,2,56,896]{4,3,2,1,0:T(8,128)} fusion(bf16[4,2,4,2,56,896]{5,4,3,2,1,0:T(8,128)(2,1)} %all-to-all-done), kind=kLoop, calls=%fused_computation.8 | loop fusion | flops 3211264 | bytes 19267584 | tf_op jit(solution)/shard_map/convert_element_type | solution.py:81
  494.7 133.2 %all-to-all-done.4 = bf16[16,4,1,56,896]{4,3,1,2,0:T(8,128)(2,1)} async-done(((bf16[16,4,1,56,896]{4,3,1,2,0:T(8,128)(2,1)}), bf16[16,4,1,56,896]{4,3,1,2,0:T(8,128)(2,1)}, u32[]{:S(2)}, u32[]{:S(2)}) %all-to-all-start.4) | async-done | bytes 6422560 | tf_op jit(solution)/shard_map/all_to_all | solution.py:71
  628.0 11.1 %copy.48 = bf16[4,2,2,4,1,56,896]{6,1,0,5,2,3,4:T(2,128)(2,1)} copy(bf16[4,2,2,4,1,56,896]{6,5,3,2,1,0,4:T(8,128)(2,1)} %bitcast.18) | data formatting | bytes 12845056 | tf_op jit(solution)/shard_map/reshape | solution.py:78
  639.0 13.9 %reshape.76 = bf16[8,4,2,56,896]{4,0,3,2,1:T(8,128)(2,1)} reshape(bf16[4,2,1,4,2,56,896]{6,1,0,5,4,3,2:T(2,128)(2,1)} %bitcast.69) | data formatting | bytes 12845056 | tf_op jit(solution)/shard_map/reshape | solution.py:79
  652.9 16.7 %fusion = bf16[8,4,2,56,896]{4,0,3,2,1:T(8,128)(2,1)} fusion(f32[8,4,2,56,896]{4,3,2,1,0:T(8,128)} %bitcast_convert_fusion, bf16[8,4,2,56,896]{4,0,3,2,1:T(8,128)(2,1)} %reshape.76, f32[8]{0:T(128)S(1)} %iota_multiply_fusion), kind=kOutput, calls=%fused_computation.2 | convolution fusion | flops 57803072 | bytes 25690144 | tf_op jit(solution)/shard_map/rk,ktlpq->rtlpq/dot_general | solution.py:80
  669.6 0.0 copy-start.2
  669.6 12.0 %multiply_reduce_fusion = f32[8,4,1024]{2,1,0:T(4,128)} fusion(f32[2,56,1024]{2,1,0:T(8,128)S(1)} %bitcast_convert_fusion.1, bf16[8,4,2,56,896]{4,0,3,2,1:T(8,128)(2,1)} %fusion, bf16[896,1024]{1,0:T(8,128)(2,1)S(1)} %copy-done), kind=kOutput, calls=%fused_computation | convolution fusion | flops 6583975936 | bytes 8847360 | tf_op jit(solution)/shard_map/rtlpq,qn->rtlpn/dot_general | solution.py:86
  681.6 0.0 all-reduce.3.cloned.1.call-update
  681.6 0.0 reduce-scatter.4.cloned.1.call-start
  681.7 0.0 copy-done.2
  681.7 0.6 dynamic-slice
  682.9 29.3 %all-reduce.3.cloned.1.call-done = f32[8,4,1024]{2,1,0:T(4,128)} async-done(((f32[8,4,1024]{2,1,0:T(4,128)}), f32[8,4,1024]{2,1,0:T(4,128)}) %all-reduce.3.cloned.1.call-update) | async-done | bytes 131088
  712.3 0.8 constant_dynamic-slice_fusion
  713.0 0.5 copy.39
  713.6 1.4 reshape.83
  715.0 0.0 reduce-scatter.4.cloned.1.call-update
  715.0 14.8 %reduce-scatter.4.cloned.1.call-done = f32[512,8]{1,0:T(8,128)} async-done(((f32[1024,8]{1,0:T(8,128)}), f32[512,8]{1,0:T(8,128)}) %reduce-scatter.4.cloned.1.call-update) | async-done | bytes 16400
  729.8 1.3 reshape.84
  731.0 0.8 copy.40
  (3 shorter events, 0.1 us)
Async XLA Ops:
  6.5 479.5 %copy-start = (bf16[896,1024]{1,0:T(8,128)(2,1)S(1)}, bf16[896,1024]{1,0:T(8,128)(2,1)}, u32[]{:S(2)}) copy-start(bf16[896,1024]{1,0:T(8,128)(2,1)} %param.5) | copy-start | bytes 5505028
  17.1 147.9 %all-to-all-start.1 = ((bf16[4,4,224,896]{3,1,2,0:T(4,128)(2,1)}), bf16[4,4,224,896]{3,1,2,0:T(4,128)(2,1)}, u32[]{:S(2)}, u32[]{:S(2)}) async-start(bf16[4,4,224,896]{3,1,2,0:T(4,128)(2,1)} %bitcast.66), calls=%async_computation.1 | async-start | bytes 12845056 | tf_op jit(solution)/shard_map/all_to_all | solution.py:56
  264.7 2.6 copy-start.1
  328.6 75.0 %all-to-all-start.3 = ((bf16[4,896,896]{2,0,1:T(4,128)(2,1)}), bf16[4,896,896]{2,0,1:T(4,128)(2,1)}, u32[]{:S(2)}, u32[]{:S(2)}) async-start(bf16[4,896,896]{2,0,1:T(4,128)(2,1)} %copy.30), calls=%async_computation.3 | async-start | bytes 12845056 | tf_op jit(solution)/shard_map/all_to_all | solution.py:62
  403.6 77.6 %all-to-all-start = ((bf16[4,2,4,2,56,896]{5,4,3,2,1,0:T(8,128)(2,1)}), bf16[4,2,4,2,56,896]{5,4,3,2,1,0:T(8,128)(2,1)}, u32[]{:S(2)}, u32[]{:S(2)}) async-start(bf16[4,2,4,2,56,896]{5,4,3,2,1,0:T(8,128)(2,1)} %copy.24), calls=%async_computation | async-start | bytes 12845056 | tf_op jit(solution)/shard_map/all_to_all | solution.py:51
  481.2 146.7 %all-to-all-start.4 = ((bf16[16,4,1,56,896]{4,3,1,2,0:T(8,128)(2,1)}), bf16[16,4,1,56,896]{4,3,1,2,0:T(8,128)(2,1)}, u32[]{:S(2)}, u32[]{:S(2)}) async-start(bf16[16,4,1,56,896]{4,3,1,2,0:T(8,128)(2,1)} %bitcast.65), calls=%async_computation.4 | async-start | bytes 12845056 | tf_op jit(solution)/shard_map/all_to_all | solution.py:71
  485.9 226.3 %all-reduce.3.cloned.1.call-start = ((), (), s32[]{:S(2)}) async-start(), calls=%async_computation.7 | async-start | bytes 262144
  669.6 12.1 %copy-start.2 = (u32[32]{0:T(128)S(1)}, u32[32]{0:T(128)}, u32[]{:S(2)}) copy-start(u32[32]{0:T(128)} %constant.44) | copy-start | bytes 388
  681.6 48.1 %reduce-scatter.4.cloned.1.call-start = ((), (), s32[]{:S(2)}) async-start(), calls=%async_computation.6 | async-start | bytes 786432
Sparse Core Ops, SparseCore 0:
  681.8 30.4 all-reduce.2
  715.1 14.6 reduce-scatter.3
where the time goes:
time: 749 us; the launch traced here: 739 us
  waiting for transfers between devices  410 us (55%)
  local copies, waits for them, and re-layouts  118 us (16%)
  matrix products  91.6 us (12%)
  blocking collectives  74.2 us (10%)
  starting transfers between devices  21.9 us (3%)
  between operations  14.4 us (2%)
  other arithmetic  8.66 us (1%)
    all_to_all x1, waiting for transfers between devices, local(): lax.all_to_all(blocks, ('th', 'tl'), split_axis=0, concat_axis=0, tiled=T...  142 us
    all_to_all x1, waiting for transfers between devices, local(): lax.all_to_all(timed, ('mom', 'th', 'tl'), split_axis=0, concat_axis=0, t...  133 us
    all_to_all x1, blocking collectives, local(): lax.all_to_all(mixed, ('pt', 'tl'), split_axis=0, concat_axis=1, tiled=True)  74.2 us
    all_to_all x1, waiting for transfers between devices, local(): lax.all_to_all(screened, ('pt', 'tl'), split_axis=1, concat_axis=0, tiled...  63.6 us
    dot_general x3, matrix products, product(): jnp.einsum('apq,aqs->aps', left, right, preferred_element_type=jnp.float32)  50.8 us
    unnamed x4, waiting for transfers between devices  44.1 us
    all_to_all x1, waiting for transfers between devices, local(): lax.all_to_all(spread, 'mom', split_axis=0, concat_axis=0, tiled=True)  27.5 us
    reshape x2, local copies, waits for them, and re-layouts, local(): timed = timed.reshape(high * low, times_dev, own_k, momenta, piece, points)  18.4 us
  transfers between devices with their start and end apart: 6, of which 6 were waited for; matrix products, arithmetic and copies ran while one was open for 8% of the time, Pallas kernels for 0%

commit v1 on v0

v1 whole, which is shorter than its diff:
```python
import functools
import math

import jax
import jax.numpy as jnp
import numpy as np
from jax import lax
from jax.experimental import pallas as pl
from jax.experimental.pallas import tpu as pltpu
from jax.sharding import PartitionSpec as P

COUPLING = 0.8
MESH = pl.DeviceIdType.MESH
BF16, F32 = jnp.bfloat16, jnp.float32


def cosine_table(count):
    index = np.arange(count, dtype=np.float64) + 0.5
    angle = np.pi * index[:, None] * index[None, :] / count
    return (np.sqrt(2.0 / count) * np.cos(angle)).astype(np.float32).astype(BF16)


def hartley_table(count):
    index = np.arange(count, dtype=np.float64)
    angle = 2.0 * np.pi * index[:, None] * index[None, :] / count
    return ((np.cos(angle) + np.sin(angle)) / np.sqrt(count)).astype(np.float32).astype(BF16)


def spread_table(table, rows):
    return jnp.asarray(np.kron(table.astype(np.float32), np.eye(rows, dtype=np.float32)).astype(BF16))


def group_rows(rows, largest):
    size = largest
    while rows % size:
        size //= 2
    return size


def flip(index, bits, count):
    total, place = 0, 1
    while place < count:
        bit = (index // place) % 2
        total = total + place * ((1 - bit) if (bits // place) % 2 else bit)
        place *= 2
    return total


def stacked(value):
    count, rows, width = value.shape
    if rows % 16:
        return value.astype(F32).reshape(count * rows, width).astype(BF16)
    return value.reshape(count * rows, width)


def dot(left, right):
    return jnp.dot(left, right, preferred_element_type=F32)


def kernel(dims, chi, green, band, mixer, turner, out, raw, mix, tiles, four, fourth, square, lat,
           cells, total, part, gathered, send1, recv1, send_g, recv_g, send2, recv2, send3, recv3,
           send4, recv4, send6, recv6):
    mom, tm, pt, times_dev, moms_dev, rows_dev, points, low, half, own_w, size1, size3, group, group_h = dims
    m, z, x = lax.axis_index("mom"), lax.axis_index("tm"), lax.axis_index("pt")
    ml, mh = m % low, m // low
    fan = pt * low
    seat = x * low + ml
    count_t = times_dev * tm
    chunks1, chunks3 = half // size1, half // size3
    scale = COUPLING / math.sqrt(points)

    def remote(source, target, send, recv, where):
        return pltpu.make_async_remote_copy(
            src_ref=source, dst_ref=target, send_sem=send, recv_sem=recv,
            device_id=dict(zip(("mom", "tm", "pt"), where)), device_id_type=MESH)

    def await_bytes(ref, sem):
        pltpu.make_async_copy(ref, ref, sem).wait()

    def rows(start, size):
        return pl.ds(pl.multiple_of(start, size), size)

    barrier = pltpu.get_barrier_semaphore()
    greeted = 0
    for i in range(mom):
        for j in range(tm):
            if i or j:
                pl.semaphore_signal(barrier, inc=1, device_id={
                    "mom": flip(m, i, mom), "tm": flip(z, j, tm), "pt": x}, device_id_type=MESH)
                greeted += 1
        for a in range(1, pt):
            pl.semaphore_signal(barrier, inc=1, device_id={
                "mom": flip(m, i, mom), "tm": z, "pt": flip(x, a, pt)}, device_id_type=MESH)
            greeted += 1
    pl.semaphore_wait(barrier, greeted)

    @pl.loop(0, chunks1)
    def _(c):
        for kl in range(moms_dev):
            to_z = moms_dev * ml + kl
            for b in range(low):
                to_l = flip(ml, b, low)
                source = chi.at[:, kl, rows(to_l * half + c * size1, size1), :]
                target = raw.at[pl.ds(times_dev * z, times_dev), rows(c * size1, size1), :]
                move = remote(source, target, send1, recv1.at[c], (mh * low + to_l, to_z, x))
                if b:
                    move.start()
                else:
                    here = to_z == z

                    @pl.when(here)
                    def _():
                        pltpu.make_async_copy(source, target, recv1.at[c]).start()

                    @pl.when(jnp.logical_not(here))
                    def _():
                        move.start()

    for i in range(mom):
        to_m = flip(m, i, mom)
        source = green.at[:, to_m]
        target = cells.at[pl.ds(moms_dev * m, moms_dev)]
        if i:
            remote(source, target, send_g, recv_g, (to_m, z, x)).start()
        else:
            pltpu.make_async_copy(source, target, recv_g).start()

    @pl.loop(0, chunks1)
    def _(c):
        await_bytes(raw.at[:, rows(c * size1, size1), :], recv1.at[c])

        @pl.loop(0, size1 // group)
        def _(g):
            block = rows(c * size1 + g * group, group)
            mixed = scale * dot(mixer[...], stacked(raw[:, block, :]))
            mix[:, block, :] = mixed.reshape(count_t, group, points).astype(BF16)

        for a in reversed(range(pt)):
            for b in range(low):
                to_x, to_l = flip(x, a, pt), flip(ml, b, low)
                source = mix.at[pl.ds(own_w * (to_x * low + to_l), own_w), rows(c * size1, size1), :]
                target = tiles.at[:, rows(seat * half + c * size1, size1), :]
                if a or b:
                    remote(source, target, send2, recv2, (mh * low + to_l, z, to_x)).start()
                else:
                    pltpu.make_async_copy(source, target, recv2).start()

    await_bytes(tiles, recv2)

    step = points
    while step > 256:
        step //= 2

    @pl.loop(0, own_w)
    def _(w):
        @pl.loop(0, points // step)
        def _(r):
            block = rows(r * step, step)
            square[block, :] = dot(tiles[w, block, :], tiles[w]).astype(BF16)

        @pl.loop(0, points // step)
        def _(r):
            block = rows(r * step, step)
            second = square[block, :]
            two = (tiles[w, block, :].astype(F32) + second.astype(F32)).astype(BF16)
            both = dot(jnp.concatenate([second, two], axis=0), square[...])
            fourth[w, block, :] = both[:step].astype(BF16)
            four[w, block, :] = (two.astype(F32) + both[step:]).astype(BF16)

    @pl.loop(0, chunks3)
    def _(c):
        @pl.loop(0, own_w)
        def _(w):
            if chunks3 == 1:
                left = four[w]
                tiles[w] = (left.astype(F32) + dot(left, fourth[w])).astype(BF16)
            else:
                places = [rows(d * half + c * size3, size3) for d in range(fan)]
                left = jnp.concatenate([four[w, place, :] for place in places], axis=0)
                last = (left.astype(F32) + dot(left, fourth[w])).astype(BF16)
                for d, place in enumerate(places):
                    tiles[w, place, :] = last[d * size3:(d + 1) * size3]

        for a in reversed(range(pt)):
            for b in range(low):
                to_x, to_l = flip(x, a, pt), flip(ml, b, low)
                source = tiles.at[:, rows((to_x * low + to_l) * half + c * size3, size3), :]
                target = raw.at[pl.ds(own_w * seat, own_w), rows(c * size3, size3), :]
                if a or b:
                    remote(source, target, send3, recv3.at[c], (mh * low + to_l, z, to_x)).start()
                else:
                    pltpu.make_async_copy(source, target, recv3.at[c]).start()

    await_bytes(mix.at[pl.ds(0, count_t - own_w)], send2)

    @pl.loop(0, chunks3)
    def _(c):
        await_bytes(raw.at[:, rows(c * size3, size3), :], recv3.at[c])

        @pl.loop(0, size3 // group)
        def _(g):
            block = rows(c * size3 + g * group, group)
            timed = dot(mixer[...], stacked(raw[:, block, :]))
            mix[:, block, :] = timed.reshape(count_t, group, points).astype(BF16)

        for j in reversed(range(tm)):
            for i in range(mom):
                to_m, to_z = flip(m, i, mom), flip(z, j, tm)
                source = mix.at[times_dev * to_z + to_m, rows(c * size3, size3), :]
                target = lat.at[tm * mh + z, ml, rows(c * size3, size3), :]
                if i or j:
                    remote(source, target, send4, recv4.at[c], (to_m, to_z, x)).start()
                else:
                    pltpu.make_async_copy(source, target, recv4.at[c]).start()

    await_bytes(cells, recv_g)
    total[...] = jnp.zeros_like(total)
    count_k = moms_dev * mom
    bands = band.shape[1]

    @pl.loop(0, chunks3)
    def _(c):
        await_bytes(lat.at[:, :, rows(c * size3, size3), :], recv4.at[c])
        for side in range(low):
            @pl.loop(0, size3 // group_h)
            def _(g):
                block = rows(c * size3 + g * group_h, group_h)
                place = rows(side * half + c * size3 + g * group_h, group_h)
                own = rows(x * rows_dev + side * half + c * size3 + g * group_h, group_h)
                lattice = dot(turner[...], stacked(lat[:, side, block, :]))
                lattice = lattice.reshape(count_k, group_h, points)
                sigma = (cells[:, place, :].astype(F32) * lattice).astype(BF16)
                applied = dot(stacked(sigma), band[...])
                applied = applied.reshape(count_k, group_h, bands) * band[own, :].astype(F32)[None]
                total[...] += jnp.sum(applied.reshape(count_k, group_h // 8, 8, bands), axis=1)

    share = bands // pt
    for to_m in range(mom):
        for to_x in range(pt):
            value = total[pl.ds(moms_dev * to_m, moms_dev), :, pl.ds(to_x * share, share)]
            part[to_m * pt + to_x] = jnp.sum(value, axis=1)
    for i in range(mom):
        for a in range(pt):
            to_m, to_x = flip(m, i, mom), flip(x, a, pt)
            source, target = part.at[to_m * pt + to_x], gathered.at[m * pt + x]
            if i or a:
                remote(source, target, send6, recv6, (to_m, z, to_x)).start()
            else:
                pltpu.make_async_copy(source, target, recv6).start()
    await_bytes(gathered, recv6)
    for t in range(times_dev):
        value = gathered[t * pt]
        for a in range(1, pt):
            value = value + gathered[t * pt + a]
        out[:, t, :] = value

    stays = z // moms_dev == ml

    @pl.when(stays)
    def _():
        await_bytes(chi.at[pl.ds(0, times_dev - times_dev // (low * moms_dev))], send1)

    @pl.when(jnp.logical_not(stays))
    def _():
        await_bytes(chi, send1)

    await_bytes(green.at[:, pl.ds(0, mom - 1)], send_g)
    await_bytes(mix.at[pl.ds(0, count_t - own_w)], send3)
    await_bytes(mix.at[pl.ds(0, count_t - 1)], send4)
    await_bytes(part.at[pl.ds(0, mom * pt - 1)], send6)


def local(mom, tm, pt, chi, green, band):
    times_dev, moms_dev, rows_dev, points = chi.shape
    bands = band.shape[1]
    count_t, count_k = times_dev * tm, moms_dev * mom
    low = tm // moms_dev
    half, own_w = rows_dev // low, count_t // (pt * low)
    if times_dev != mom or low * moms_dev != tm or own_w * pt * low != count_t:
        raise ValueError("unsupported mesh")
    group = group_rows(half, 16)
    size1 = group if group == 16 else half
    group_h = group_rows(half, 32)
    size3 = group_h if group_h == 32 else half
    dims = (mom, tm, pt, times_dev, moms_dev, rows_dev, points, low, half, own_w, size1, size3, group, group_h)
    mixer = spread_table(cosine_table(count_t), group)
    turner = spread_table(hartley_table(count_k), group_h)
    dma = pltpu.SemaphoreType.DMA
    anywhere = pl.BlockSpec(memory_space=pl.ANY)
    vmem = pl.BlockSpec(memory_space=pltpu.VMEM)
    return pl.pallas_call(
        functools.partial(kernel, dims),
        out_shape=jax.ShapeDtypeStruct((moms_dev, times_dev, bands // pt), F32),
        in_specs=[anywhere, anywhere, vmem, vmem, vmem],
        out_specs=vmem,
        scratch_shapes=[
            pltpu.VMEM((count_t, half, points), BF16),
            pltpu.VMEM((count_t, half, points), BF16),
            pltpu.VMEM((own_w, points, points), BF16),
            pltpu.VMEM((own_w, points, points), BF16),
            pltpu.VMEM((own_w, points, points), BF16),
            pltpu.VMEM((points, points), BF16),
            pltpu.VMEM((count_k, low, half, points), BF16),
            pltpu.VMEM((count_k, rows_dev, points), BF16),
            pltpu.VMEM((count_k, 8, bands), F32),
            pltpu.VMEM((mom * pt, moms_dev, bands // pt), F32),
            pltpu.VMEM((mom * pt, moms_dev, bands // pt), F32),
            dma, dma((half // size1,)), dma, dma, dma, dma,
            dma, dma((half // size3,)), dma, dma((half // size3,)), dma, dma,
        ],
        compiler_params=pltpu.CompilerParams(
            collective_id=0, has_side_effects=True, vmem_limit_bytes=60 << 20),
        name="screened",
    )(chi, green, band, mixer, turner)


def solution(mesh):
    sizes = dict(mesh.shape)
    placed = (P("tm", "mom", "pt", None), P("mom", "tm", "pt", None), P())
    return jax.shard_map(
        functools.partial(local, sizes["mom"], sizes["tm"], sizes["pt"]),
        mesh=mesh, in_specs=placed, out_specs=P("mom", "tm", "pt"), check_vma=False,
    )
```

time: 749 us -> 342 us (0.46); the launches traced: 739 us -> 340 us
  waiting for transfers between devices: 410 us -> 0 us
  Pallas kernels: 0 us -> 339 us
  local copies, waits for them, and re-layouts: 118 us -> 1.32 us
  matrix products: 91.6 us -> 0 us
  blocking collectives: 74.2 us -> 0 us
  starting transfers between devices: 21.9 us -> 0 us
  between operations: 14.4 us -> 0.01 us
  other arithmetic: 8.66 us -> 0 us
    all_to_all x4 -> x0, waiting for transfers between devices: 366 us -> none  [the longest x1 142 us: local(): lax.all_to_all(blocks, ('th', 'tl'), split_axis=0, concat_axis=0, tiled=T...]
    pallas_call x0 -> x1, Pallas kernels: none -> 339 us  [local(): pl.pallas_call(functools.partial(kernel, dims), out_shape=jax.ShapeDtypeS...]
    dot_general x7 -> x0, matrix products: 91.6 us -> none  [the longest x3 50.8 us: product(): jnp.einsum('apq,aqs->aps', left, right, preferred_element_type=jnp.float32)]
    all_to_all x1 -> x0, blocking collectives: 74.2 us -> none  [local(): lax.all_to_all(mixed, ('pt', 'tl'), split_axis=0, concat_axis=1, tiled=True)]
    reshape x6 -> x0, local copies, waits for them, and re-layouts: 64.9 us -> none  [the longest x2 18.4 us: local(): timed = timed.reshape(high * low, times_dev, own_k, momenta, piece, points)]
    unnamed x4 -> x0, waiting for transfers between devices: 44.1 us -> none
    all_to_all x4 -> x0, starting transfers between devices: 21.8 us -> none  [the longest x1 6.35 us: local(): lax.all_to_all(blocks, ('th', 'tl'), split_axis=0, concat_axis=0, tiled=T...]
    all_to_all x3 -> x0, local copies, waits for them, and re-layouts: 16.1 us -> none  [the longest x1 7.73 us: local(): lax.all_to_all(screened, ('pt', 'tl'), split_axis=1, concat_axis=0, tiled...]
  transfers between devices with their start and end apart: 6 -> 0, of which waited for: 6 -> 0; matrix products, arithmetic and copies ran while one was open for 8% -> 0% of each run, Pallas kernels for 0% -> 0%
where the time goes in v1:
time: 342 us; the launch traced here: 340 us
  Pallas kernels  339 us (99%)
    pallas_call x1, Pallas kernels, local(): pl.pallas_call(functools.partial(kernel, dims), out_shape=jax.ShapeDtypeS...  339 us

profile of v1, /device:TPU:0, one launch (start us, length us, event | category | flops | bytes accessed | tf_op | source)
XLA Modules:
  0.0 339.9 jit_solution(3561300068214242762)
XLA Ops:
  0.0 338.5 %screened.1 = f32[2,4,512]{2,1,0:T(4,128)} custom-call(bf16[4,2,448,896]{3,2,1,0:T(8,128)(2,1)} %chi.1, bf16[2,4,448,896]{3,2,1,0:T(8,128)(2,1)} %green.1, bf16[896,1024]{1,0:T(8,128)(2,1)} %band.1, bf16[256,256]{1,0:T(8,128)(2,1)} %constant.4.clone.mixer, bf16[256,256]{1,0:T(8,128)(2,1)} %constant.5.clone.turner), custom_call_target="tpu_custom_call" | custom-call | tf_op jit(solution)/shard_map/screened/pallas_call | solution.py:291
  338.6 1.3 copy.7

commit v2 on v1

--- a/solution.py
+++ b/solution.py
@@ -10,6 +10,7 @@
 from jax.sharding import PartitionSpec as P
 
 COUPLING = 0.8
+WINDOW = 3
 MESH = pl.DeviceIdType.MESH
 BF16, F32 = jnp.bfloat16, jnp.float32
 
@@ -59,7 +60,7 @@
 
 def kernel(dims, chi, green, band, mixer, turner, out, raw, mix, tiles, four, fourth, square, lat,
            cells, total, part, gathered, send1, recv1, send_g, recv_g, send2, recv2, send3, recv3,
-           send4, recv4, send6, recv6):
+           send4, recv4, send6, recv6, credit_end, credit_mid):
     mom, tm, pt, times_dev, moms_dev, rows_dev, points, low, half, own_w, size1, size3, group, group_h = dims
     m, z, x = lax.axis_index("mom"), lax.axis_index("tm"), lax.axis_index("pt")
     ml, mh = m % low, m // low
@@ -94,27 +95,26 @@
             greeted += 1
     pl.semaphore_wait(barrier, greeted)
 
-    @pl.loop(0, chunks1)
-    def _(c):
-        for kl in range(moms_dev):
-            to_z = moms_dev * ml + kl
-            for b in range(low):
-                to_l = flip(ml, b, low)
-                source = chi.at[:, kl, rows(to_l * half + c * size1, size1), :]
-                target = raw.at[pl.ds(times_dev * z, times_dev), rows(c * size1, size1), :]
-                move = remote(source, target, send1, recv1.at[c], (mh * low + to_l, to_z, x))
-                if b:
+    def send_times(c, late):
+        kl = 1 - ml if late else ml
+        to_z = moms_dev * ml + kl
+        for b in range(low):
+            to_l = flip(ml, b, low)
+            source = chi.at[:, kl, rows(to_l * half + c * size1, size1), :]
+            target = raw.at[pl.ds(times_dev * z, times_dev), rows(c * size1, size1), :]
+            move = remote(source, target, send1, recv1.at[c], (mh * low + to_l, to_z, x))
+            if b:
+                move.start()
+            else:
+                here = to_z == z
+
+                @pl.when(here)
+                def _():
+                    pltpu.make_async_copy(source, target, recv1.at[c]).start()
+
+                @pl.when(jnp.logical_not(here))
+                def _():
                     move.start()
-                else:
-                    here = to_z == z
-
-                    @pl.when(here)
-                    def _():
-                        pltpu.make_async_copy(source, target, recv1.at[c]).start()
-
-                    @pl.when(jnp.logical_not(here))
-                    def _():
-                        move.start()
 
     for i in range(mom):
         to_m = flip(m, i, mom)
@@ -125,9 +125,26 @@
         else:
             pltpu.make_async_copy(source, target, recv_g).start()
 
-    @pl.loop(0, chunks1)
-    def _(c):
+    at_end = z % (tm - 1) == 0
+    window = min(WINDOW, chunks1)
+
+    def mix_times(c):
         await_bytes(raw.at[:, rows(c * size1, size1), :], recv1.at[c])
+
+        @pl.when(c < chunks1 - window)
+        def _():
+            for from_z in range(1, tm - 1):
+                from_m = mh * low + z // moms_dev
+                mine = jnp.logical_and(from_z == z, from_m == m)
+                for sem, which in ((credit_end, at_end), (credit_mid, jnp.logical_not(at_end))):
+                    @pl.when(jnp.logical_and(which, mine))
+                    def _():
+                        pl.semaphore_signal(sem.at[ml], inc=1)
+
+                    @pl.when(jnp.logical_and(which, jnp.logical_not(mine)))
+                    def _():
+                        pl.semaphore_signal(sem.at[ml], inc=1, device_id={
+                            "mom": from_m, "tm": from_z, "pt": x}, device_id_type=MESH)
 
         @pl.loop(0, size1 // group)
         def _(g):
@@ -144,6 +161,54 @@
                     remote(source, target, send2, recv2, (mh * low + to_l, z, to_x)).start()
                 else:
                     pltpu.make_async_copy(source, target, recv2).start()
+
+    @pl.when(at_end)
+    def _():
+        @pl.loop(0, chunks1)
+        def _(c):
+            send_times(c, False)
+
+            @pl.when(c % 2 == 1)
+            def _():
+                send_times(c // 2, True)
+
+        @pl.loop(chunks1 // 2, chunks1)
+        def _(c):
+            send_times(c, True)
+
+        @pl.loop(0, chunks1)
+        def _(c):
+            mix_times(c)
+
+    @pl.when(jnp.logical_not(at_end))
+    def _():
+        def late(c):
+            @pl.when(c >= window)
+            def _():
+                mix_times(c - window)
+                for b in range(low):
+                    pl.semaphore_wait(credit_mid.at[b], 1)
+            send_times(c, True)
+
+        @pl.loop(0, chunks1)
+        def _(c):
+            @pl.when(c >= window)
+            def _():
+                for b in range(low):
+                    pl.semaphore_wait(credit_end.at[b], 1)
+            send_times(c, False)
+
+            @pl.when(c % 2 == 1)
+            def _():
+                late(c // 2)
+
+        @pl.loop(chunks1 // 2, chunks1)
+        def _(c):
+            late(c)
+
+        @pl.loop(chunks1 - window, chunks1)
+        def _(c):
+            mix_times(c)
 
     await_bytes(tiles, recv2)
 
@@ -193,6 +258,16 @@
 
     await_bytes(mix.at[pl.ds(0, count_t - own_w)], send2)
 
+    def send_cells(c, j):
+        for i in range(mom):
+            to_m, to_z = flip(m, i, mom), flip(z, j, tm)
+            source = mix.at[times_dev * to_z + to_m, rows(c * size3, size3), :]
+            target = lat.at[tm * mh + z, ml, rows(c * size3, size3), :]
+            if i or j:
+                remote(source, target, send4, recv4.at[c], (to_m, to_z, x)).start()
+            else:
+                pltpu.make_async_copy(source, target, recv4.at[c]).start()
+
     @pl.loop(0, chunks3)
     def _(c):
         await_bytes(raw.at[:, rows(c * size3, size3), :], recv3.at[c])
@@ -204,14 +279,18 @@
             mix[:, block, :] = timed.reshape(count_t, group, points).astype(BF16)
 
         for j in reversed(range(tm)):
-            for i in range(mom):
-                to_m, to_z = flip(m, i, mom), flip(z, j, tm)
-                source = mix.at[times_dev * to_z + to_m, rows(c * size3, size3), :]
-                target = lat.at[tm * mh + z, ml, rows(c * size3, size3), :]
-                if i or j:
-                    remote(source, target, send4, recv4.at[c], (to_m, to_z, x)).start()
-                else:
-                    pltpu.make_async_copy(source, target, recv4.at[c]).start()
+            if j == 1:
+                @pl.when(jnp.logical_not(at_end))
+                def _():
+                    send_cells(c, 1)
+            else:
+                send_cells(c, j)
+
+    @pl.when(at_end)
+    def _():
+        @pl.loop(0, chunks3)
+        def _(c):
+            send_cells(c, 1)
 
     await_bytes(cells, recv_g)
     total[...] = jnp.zeros_like(total)
@@ -276,7 +355,7 @@
     count_t, count_k = times_dev * tm, moms_dev * mom
     low = tm // moms_dev
     half, own_w = rows_dev // low, count_t // (pt * low)
-    if times_dev != mom or low * moms_dev != tm or own_w * pt * low != count_t:
+    if times_dev != mom or low != 2 or low * moms_dev != tm or own_w * pt * low != count_t:
         raise ValueError("unsupported mesh")
     group = group_rows(half, 16)
     size1 = group if group == 16 else half
@@ -307,6 +386,7 @@
             pltpu.VMEM((mom * pt, moms_dev, bands // pt), F32),
             dma, dma((half // size1,)), dma, dma, dma, dma,
             dma, dma((half // size3,)), dma, dma((half // size3,)), dma, dma,
+            pltpu.SemaphoreType.REGULAR((low,)), pltpu.SemaphoreType.REGULAR((low,)),
         ],
         compiler_params=pltpu.CompilerParams(
             collective_id=0, has_side_effects=True, vmem_limit_bytes=60 << 20),

time: 342 us -> 329 us (0.962)
  Pallas kernels: 339 us -> 327 us
    pallas_call x1, Pallas kernels: 339 us -> 327 us  [local(): pl.pallas_call(functools.partial(kernel, dims), out_shape=jax.ShapeDtypeS...]
where the time goes in v2:
time: 329 us; the launch traced here: 328 us
  Pallas kernels  327 us (99%)
    pallas_call x1, Pallas kernels, local(): pl.pallas_call(functools.partial(kernel, dims), out_shape=jax.ShapeDtypeS...  327 us

profile of v2, /device:TPU:0, one launch (start us, length us, event | category | flops | bytes accessed | tf_op | source)
XLA Modules:
  0.0 328.4 jit_solution(6468938033498272536)
XLA Ops:
  0.0 327.1 %screened.1 = f32[2,4,512]{2,1,0:T(4,128)} custom-call(bf16[4,2,448,896]{3,2,1,0:T(8,128)(2,1)} %chi.1, bf16[2,4,448,896]{3,2,1,0:T(8,128)(2,1)} %green.1, bf16[896,1024]{1,0:T(8,128)(2,1)} %band.1, bf16[256,256]{1,0:T(8,128)(2,1)} %constant.4.clone.mixer, bf16[256,256]{1,0:T(8,128)(2,1)} %constant.5.clone.turner), custom_call_target="tpu_custom_call" | custom-call | tf_op jit(solution)/shard_map/screened/pallas_call | solution.py:370
  327.1 1.3 copy.7

commit v3 on v2

--- a/solution.py
+++ b/solution.py
@@ -213,7 +213,7 @@
     await_bytes(tiles, recv2)
 
     step = points
-    while step > 256:
+    while step > 512:
         step //= 2
 
     @pl.loop(0, own_w)

time: 329 us -> 326 us (level)
  no operation moved by 1% of the time
where the time goes in v3:
time: 326 us
  Pallas kernels  324 us (99%)
    pallas_call x1, Pallas kernels, local(): pl.pallas_call(functools.partial(kernel, dims), out_shape=jax.ShapeDtypeS...  324 us

profile of v3, /device:TPU:0, one launch (start us, length us, event | category | flops | bytes accessed | tf_op | source)
XLA Modules:
  0.0 325.5 jit_solution(5260692351109425805)
XLA Ops:
  0.0 324.2 %screened.1 = f32[2,4,512]{2,1,0:T(4,128)} custom-call(bf16[4,2,448,896]{3,2,1,0:T(8,128)(2,1)} %chi.1, bf16[2,4,448,896]{3,2,1,0:T(8,128)(2,1)} %green.1, bf16[896,1024]{1,0:T(8,128)(2,1)} %band.1, bf16[256,256]{1,0:T(8,128)(2,1)} %constant.4.clone.mixer, bf16[256,256]{1,0:T(8,128)(2,1)} %constant.5.clone.turner), custom_call_target="tpu_custom_call" | custom-call | tf_op jit(solution)/shard_map/screened/pallas_call | solution.py:370
  324.2 1.3 copy.7
